TPU v7x, 32 devices: a whole 2x2x4 slice. The times are simulated.
32 devices in a mesh: rep: 8 (over z, y), shard: 4 (over x, core).
Axes of the slice: x: 2, y: 2, z: 4, core: 2. Of those that a mesh axis runs over, the one named last changes fastest.
Arguments:
- activ: bfloat16 [4096, 8192], P(('rep', 'shard')), may hold values from -6 to 6
- key_grad: bfloat16 [4096, 640], P(('rep', 'shard')), may hold values from -1.1953125 to 1.1953125
- key_weight: bfloat16 [8192, 640], P('shard'), may hold values from -0.25 to 0.25
- feedback: bfloat16 [8, 40960, 128], P('rep', 'shard'), may hold values from -24 to 24
- kept: int32 [8, 4, 512], P('rep', 'shard'), may hold values from 0 to 10239, as said below
- region_len: int32 [4, 8], P('shard'), may hold values from 640 to 1920, as said below
Outputs:
- input_grad: bfloat16 [4096, 8192], P(('rep', 'shard'))
- next_feedback: bfloat16 [8, 40960, 128], P('rep', 'shard')
- owned_sum: float32 [4, 15360, 128], P('shard', 'rep')
Inputs may be any that keep to these rules, and one draw needn't show every extreme that they name: `region_len`: each row splits its shard's 10240 blocks into 8 regions in order of owner and sums to 10240; every row has a region of exactly 1920 blocks. `kept`: the 512 numbers of a row are different blocks of that shard. At most 128 of them lie in one region of the shard; every row has exactly 128 in some region, and in every shard some region gets exactly 128 from every replica.
All inputs are finite; a program needn't handle non-finite values.
Results may differ from a plain program's by a relative error of at most 0.011.
Values may be sent and summed in bfloat16 or wider, within the bound.
A program may use at most 128 MiB of HBM per device.

v0:
```python
import jax
import jax.numpy as jnp
from jax import lax
from jax.sharding import PartitionSpec as P


def accumulate(block_rows, block_ids, own_start, own_len, region_max):
    offset = block_ids - own_start
    inside = (offset >= 0) & (offset < own_len)
    target = jnp.where(inside, offset, region_max)
    blank = jnp.zeros((region_max, block_rows.shape[1]), jnp.float32)
    return blank.at[target].add(block_rows.astype(jnp.float32), mode="drop")


def per_device(activ, key_grad, key_weight, feedback, kept, region_len):
    grads_all = lax.all_gather(key_grad, "shard", axis=0, tiled=True)
    act_cols = lax.all_to_all(activ, "shard", split_axis=1, concat_axis=0, tiled=True)
    weight_grad = lax.dot_general(
        act_cols, grads_all, (((0,), (0,)), ((), ())), preferred_element_type=jnp.float32
    )
    input_cols = lax.dot_general(
        grads_all, key_weight, (((1,), (1,)), ((), ())), preferred_element_type=jnp.float32
    ).astype(jnp.bfloat16)
    input_grad = lax.all_to_all(input_cols, "shard", split_axis=0, concat_axis=1, tiled=True)
    table = feedback[0]
    chosen = kept[0, 0]
    lengths = region_len[0]
    replicas = lax.axis_size("rep")
    block_count = table.shape[0]
    block_size = table.shape[1]
    keep_count = chosen.shape[0]
    mean_len = block_count // replicas
    region_max = mean_len + mean_len // 2
    starts = jnp.cumsum(lengths) - lengths
    owner_self = lax.axis_index("rep")
    own_start = starts[owner_self]
    own_len = lengths[owner_self]
    kept_rows = table[chosen]
    flags = jnp.zeros((block_count,), bool).at[chosen].set(True)
    cleared = jnp.where(flags[:, None], jnp.float32(0.0), table.astype(jnp.float32))
    next_feedback = (cleared + weight_grad.reshape(block_count, block_size)).astype(jnp.bfloat16)[
        None
    ]
    owner_id = jnp.sum((starts[None, :] <= chosen[:, None]).astype(jnp.int32), axis=1) - 1
    serial = jnp.arange(keep_count, dtype=jnp.int32)
    earlier = (owner_id[:, None] == owner_id[None, :]) & (serial[None, :] < serial[:, None])
    slot_index = jnp.sum(earlier.astype(jnp.int32), axis=1)
    capacity = 2 * keep_count // replicas
    place_at = owner_id * capacity + slot_index
    send_rows = (
        jnp.zeros((replicas * capacity, block_size), jnp.bfloat16).at[place_at].set(kept_rows)
    )
    send_ids = jnp.full((replicas * capacity,), -1, jnp.int32).at[place_at].set(chosen)
    got_rows, got_ids = (
        lax.all_to_all(send_rows, "rep", split_axis=0, concat_axis=0, tiled=True),
        lax.all_to_all(send_ids, "rep", split_axis=0, concat_axis=0, tiled=True),
    )
    owned_rows = accumulate(got_rows, got_ids, own_start, own_len, region_max)
    return (input_grad, next_feedback, owned_rows[None])


def solution(mesh):
    return jax.shard_map(
        per_device,
        mesh=mesh,
        in_specs=(
            P(("rep", "shard"), None),
            P(("rep", "shard"), None),
            P("shard", None),
            P("rep", "shard", None),
            P("rep", "shard", None),
            P("shard", None),
        ),
        out_specs=(P(("rep", "shard"), None), P("rep", "shard", None), P("shard", "rep", None)),
        check_vma=False,
    )
```

profile of v0, /device:TPU:0, one launch (start us, length us, event | category | flops | bytes accessed | tf_op | source)
XLA Modules:
  0.0 117.7 jit_solution(1622688939139694994)
XLA Ops:
  0.6 0.0 copy-start
  0.6 1.0 reduce-window.4
  1.6 0.7 fusion.11
  2.3 0.8 convert_reduce_fusion.1
  3.1 0.3 convert_reduce_fusion
  3.3 3.2 %scatter_custom_fusion.1 = s32[1024]{0:T(1024)} fusion(s32[512]{0:T(512)S(1)} %bitcast.56, s32[512]{0:T(512)} %bitcast.54, s32[]{:T(128)} %constant.18.clone.1), kind=kCustom, calls=%fused_computation.26 | custom fusion | bytes 4608 | tf_op jit(solution)/shard_map/scatter | solution.py:53
  6.5 7.3 %all-to-all-start.2 = ((s32[8,128,1]{1,2,0:T(1,128)}), s32[8,128,1]{1,2,0:T(1,128)S(1)}, u32[]{:S(2)}, u32[]{:S(2)}) async-start(s32[8,128,1]{1,2,0:T(1,128)} %bitcast.14), calls=%async_computation.2 | async-start | bytes 8192 | tf_op jit(solution)/shard_map/all_to_all | solution.py:56
  13.8 0.7 compare_select_fusion.2
  14.5 0.0 copy-start.2
  14.5 0.6 copy-done.2
  15.1 5.5 %scatter_custom_fusion.2 = bf16[1024,128]{1,0:T(8,128)(2,1)} fusion(s32[512]{0:T(512)S(1)} %bitcast.57, bf16[]{:T(256)} %constant.12.clone.1, bf16[10240,128]{1,0:T(8,128)(2,1)} %bitcast.43, s32[1024]{0:T(1024)S(1)} %pad_clamp_fusion), kind=kCustom, calls=%fused_computation.13 | custom fusion | bytes 262656 | tf_op jit(solution)/shard_map/scatter | solution.py:51
  20.6 0.0 all-to-all-done.2
  20.6 6.0 %all-to-all-start.3 = ((bf16[8,128,128]{2,1,0:T(8,128)(2,1)}), bf16[8,128,128]{2,1,0:T(8,128)(2,1)S(1)}, u32[]{:S(2)}, u32[]{:S(2)}) async-start(bf16[8,128,128]{2,1,0:T(8,128)(2,1)} %bitcast.23), calls=%async_computation.3 | async-start | bytes 524288 | tf_op jit(solution)/shard_map/all_to_all | solution.py:55
  26.6 4.1 %copy.20 = bf16[128,8192]{0,1:T(8,128)(2,1)} copy(bf16[128,8192]{1,0:T(8,128)(2,1)} %param.6) | data formatting | bytes 4194304 | tf_op args[0]
  30.7 4.4 %all-to-all-done.3 = bf16[8,128,128]{2,1,0:T(8,128)(2,1)S(1)} async-done(((bf16[8,128,128]{2,1,0:T(8,128)(2,1)}), bf16[8,128,128]{2,1,0:T(8,128)(2,1)S(1)}, u32[]{:S(2)}, u32[]{:S(2)}) %all-to-all-start.3) | async-done | bytes 262176 | tf_op jit(solution)/shard_map/all_to_all | solution.py:55
  35.1 4.4 %all-to-all-start.1 = ((bf16[128,4,2048]{0,2,1:T(8,128)(2,1)}), bf16[128,4,2048]{0,2,1:T(8,128)(2,1)}, u32[]{:S(2)}, u32[]{:S(2)}) async-start(bf16[128,4,2048]{0,2,1:T(8,128)(2,1)} %bitcast.42), calls=%async_computation.1 | async-start | bytes 4194304 | tf_op jit(solution)/shard_map/all_to_all | solution.py:17
  39.6 30.0 %all_gather.3 = bf16[512,640]{1,0:T(8,128)(2,1)S(1)} all-gather(bf16[128,640]{1,0:T(8,128)(2,1)} %param.7), channel_id=1, replica_groups=mesh['rep'=8,'shard'=4] {'shard'}, dimensions={0}, use_global_device_ids=true | all-gather | bytes 819200 | tf_op jit(solution)/shard_map/all_gather | solution.py:16
  69.6 0.0 copy-done
  69.6 3.1 %convolution_convert_fusion = bf16[512,2048]{1,0:T(8,128)(2,1)} fusion(bf16[512,640]{1,0:T(8,128)(2,1)S(1)} %all_gather.3, bf16[2048,640]{1,0:T(8,128)(2,1)S(1)} %copy-done), kind=kOutput, calls=%fused_computation.6 | convolution fusion | flops 1343225856 | bytes 5373952 | tf_op jit(solution)/shard_map/dot_general | solution.py:21
  72.7 0.0 copy-start.3
  72.7 0.0 all-to-all-done.1
  72.7 4.6 %all-to-all-start = ((bf16[4,128,2048]{2,1,0:T(8,128)(2,1)}), bf16[4,128,2048]{2,1,0:T(8,128)(2,1)}, u32[]{:S(2)}, u32[]{:S(2)}) async-start(bf16[4,128,2048]{2,1,0:T(8,128)(2,1)} %bitcast.44), calls=%async_computation | async-start | bytes 4194304 | tf_op jit(solution)/shard_map/all_to_all | solution.py:24
  77.4 0.0 copy-done.3
  77.4 0.6 constant_dynamic-slice_fusion
  78.0 0.6 dynamic_slice.6
  78.6 0.5 broadcast.121
  79.1 2.6 %scatter_custom_fusion = pred[10240]{0:T(1024)(128)(4,1)S(1)} fusion(s32[512]{0:T(512)} %bitcast.51, pred[512]{0:T(512)(128)(4,1)} %broadcast.121, pred[]{:T(512)} %constant.13.clone.1), kind=kCustom, calls=%fused_computation.17 | custom fusion | bytes 10752 | tf_op jit(solution)/shard_map/scatter | solution.py:39
  81.7 0.7 broadcast_subtract_fusion
  82.3 0.6 compare_select_fusion
  83.0 7.0 %scatter_custom_fusion.3 = f32[1920,128]{1,0:T(8,128)} fusion(s32[1024]{0:T(1024)S(1)} %bitcast.55, bf16[1024,128]{1,0:T(8,128)(2,1)S(1)} %bitcast.46, f32[]{:T(128)} %constant.17.clone.1), kind=kCustom, calls=%fused_computation.10 | custom fusion | flops 262144 | bytes 1245188 | tf_op jit(solution)/shard_map/scatter-add | solution.py:12
  90.0 3.9 %copy.21 = bf16[4,128,2048]{2,1,0:T(8,128)(2,1)} copy(bf16[4,128,2048]{1,2,0:T(8,128)(2,1)} %bitcast.5) | data formatting | bytes 4194304 | tf_op jit(solution)/shard_map/all_to_all | solution.py:17
  93.9 5.8 %fusion.12 = f32[2048,640]{1,0:T(8,128)} fusion(bf16[512,2048]{1,0:T(8,128)(2,1)} %bitcast.41, bf16[512,640]{1,0:T(8,128)(2,1)S(1)} %all_gather.3), kind=kOutput, calls=%fused_computation.33 | convolution fusion | flops 1342177280 | bytes 7995392 | tf_op jit(solution)/shard_map/dot_general | solution.py:18
  99.7 6.5 %reshape.138 = f32[1,10240,128]{2,1,0:T(8,128)} reshape(f32[2048,640]{1,0:T(8,128)} %fusion.12) | data formatting | bytes 10485760 | tf_op jit(solution)/shard_map/reshape | solution.py:41
  106.2 0.0 all-to-all-done
  106.2 0.0 copy-start.1
  106.2 3.3 %copy.24 = bf16[4,16,8,2048]{3,2,0,1:T(8,128)(2,1)} copy(bf16[4,16,8,2048]{3,2,1,0:T(8,128)(2,1)} %bitcast.28) | data formatting | bytes 4194304 | tf_op jit(solution)/shard_map/all_to_all | solution.py:24
  109.5 0.0 copy-done.1
  109.5 8.2 %add_convert_fusion = bf16[1,10240,128]{2,1,0:T(8,128)(2,1)} fusion(f32[1,10240,128]{2,1,0:T(8,128)} %reshape.138, bf16[1,10240,128]{2,1,0:T(8,128)(2,1)S(1)} %copy-done.1, pred[10240]{0:T(1024)(128)(4,1)S(1)} %scatter_custom_fusion), kind=kLoop, calls=%fused_computation.5 | loop fusion | flops 5242880 | bytes 10496000 | tf_op jit(solution)/shard_map/convert_element_type | solution.py:41
  (5 shorter events, 0.0 us)
Async XLA Ops:
  0.6 68.9 %copy-start = (bf16[2048,640]{1,0:T(8,128)(2,1)S(1)}, bf16[2048,640]{1,0:T(8,128)(2,1)}, u32[]{:S(2)}) copy-start(bf16[2048,640]{1,0:T(8,128)(2,1)} %param.8) | copy-start | bytes 7864324
  6.5 14.1 %all-to-all-start.2 = ((s32[8,128,1]{1,2,0:T(1,128)}), s32[8,128,1]{1,2,0:T(1,128)S(1)}, u32[]{:S(2)}, u32[]{:S(2)}) async-start(s32[8,128,1]{1,2,0:T(1,128)} %bitcast.14), calls=%async_computation.2 | async-start | bytes 8192 | tf_op jit(solution)/shard_map/all_to_all | solution.py:56
  14.5 0.6 copy-start.2
  20.6 14.5 %all-to-all-start.3 = ((bf16[8,128,128]{2,1,0:T(8,128)(2,1)}), bf16[8,128,128]{2,1,0:T(8,128)(2,1)S(1)}, u32[]{:S(2)}, u32[]{:S(2)}) async-start(bf16[8,128,128]{2,1,0:T(8,128)(2,1)} %bitcast.23), calls=%async_computation.3 | async-start | bytes 524288 | tf_op jit(solution)/shard_map/all_to_all | solution.py:55
  35.1 37.6 %all-to-all-start.1 = ((bf16[128,4,2048]{0,2,1:T(8,128)(2,1)}), bf16[128,4,2048]{0,2,1:T(8,128)(2,1)}, u32[]{:S(2)}, u32[]{:S(2)}) async-start(bf16[128,4,2048]{0,2,1:T(8,128)(2,1)} %bitcast.42), calls=%async_computation.1 | async-start | bytes 4194304 | tf_op jit(solution)/shard_map/all_to_all | solution.py:17
  72.7 4.6 %copy-start.3 = (s32[1,8]{1,0:T(1,128)S(1)}, s32[1,8]{1,0:T(1,128)}, u32[]{:S(2)}) copy-start(s32[1,8]{1,0:T(1,128)} %param.11) | copy-start | bytes 100
  72.7 33.5 %all-to-all-start = ((bf16[4,128,2048]{2,1,0:T(8,128)(2,1)}), bf16[4,128,2048]{2,1,0:T(8,128)(2,1)}, u32[]{:S(2)}, u32[]{:S(2)}) async-start(bf16[4,128,2048]{2,1,0:T(8,128)(2,1)} %bitcast.44), calls=%async_computation | async-start | bytes 4194304 | tf_op jit(solution)/shard_map/all_to_all | solution.py:24
  106.2 3.3 %copy-start.1 = (bf16[1,10240,128]{2,1,0:T(8,128)(2,1)S(1)}, bf16[1,10240,128]{2,1,0:T(8,128)(2,1)}, u32[]{:S(2)}) copy-start(bf16[1,10240,128]{2,1,0:T(8,128)(2,1)} %param.9) | copy-start | bytes 7864324
where the time goes:
time: 119 us; the launch traced here: 118 us
  local copies, waits for them, and re-layouts  31.4 us (26%)
  blocking collectives  30 us (25%)
  starting transfers between devices  22.4 us (19%)
  other arithmetic  19.8 us (17%)
  matrix products  8.92 us (7%)
  waiting for transfers between devices  4.45 us (4%)
    all_gather x1, blocking collectives, per_device(): grads_all = lax.all_gather(key_grad, 'shard', axis=0, tiled=True)  30 us
    convert_element_type x1, other arithmetic, per_device(): (cleared + weight_grad.reshape(block_count, block_size)).astype(jnp.bfloa...  8.16 us
    all_to_all x1, starting transfers between devices, per_device(): lax.all_to_all(send_ids, 'rep', split_axis=0, concat_axis=0, tiled=True)  7.31 us
    scatter-add x1, other arithmetic, accumulate(): return blank.at[target].add(block_rows.astype(jnp.float32), mode='drop')  7.02 us
    reshape x1, local copies, waits for them, and re-layouts, per_device(): weight_grad.reshape(block_count, block_size)  6.47 us
    all_to_all x1, starting transfers between devices, per_device(): lax.all_to_all(send_rows, 'rep', split_axis=0, concat_axis=0, tiled=True)  6 us
    dot_general x1, matrix products, per_device(): lax.dot_general(act_cols, grads_all, (((0,), (0,)), ((), ())), preferred_...  5.78 us
    scatter x1, local copies, waits for them, and re-layouts, per_device(): jnp.zeros((replicas * capacity, block_size), jnp.bfloat16).at[place_at]  5.51 us
  transfers between devices with their start and end apart: 4, of which 1 were waited for; matrix products, arithmetic and copies ran while one was open for 36% of the time, Pallas kernels for 0%

commit v1 on v0

--- a/solution.py
+++ b/solution.py
@@ -13,7 +13,14 @@
 
 
 def per_device(activ, key_grad, key_weight, feedback, kept, region_len):
-    grads_all = lax.all_gather(key_grad, "shard", axis=0, tiled=True)
+    ring = [key_grad]
+    for hop in range(3):
+        ring.append(lax.ppermute(ring[-1], "shard", [(dev, (dev + 1) % 4) for dev in range(4)]))
+    grads_all = jnp.roll(
+        jnp.concatenate(ring[::-1], axis=0),
+        (lax.axis_index("shard") + 1) * ring[0].shape[0],
+        axis=0,
+    )
     act_cols = lax.all_to_all(activ, "shard", split_axis=1, concat_axis=0, tiled=True)
     weight_grad = lax.dot_general(
         act_cols, grads_all, (((0,), (0,)), ((), ())), preferred_element_type=jnp.float32

time: 119 us -> 111 us (0.933)
  blocking collectives: 30 us -> 0 us
  waiting for transfers between devices: 4.45 us -> 18.7 us
  local copies, waits for them, and re-layouts: 31.4 us -> 37.2 us
  starting transfers between devices: 22.4 us -> 24.3 us
    all_gather x1 -> x0, blocking collectives: 30 us -> none  [per_device(): grads_all = lax.all_gather(key_grad, 'shard', axis=0, tiled=True)]
    ppermute x0 -> x3, waiting for transfers between devices: none -> 18.5 us  [per_device(): lax.ppermute(ring[-1], 'shard', [(dev, (dev + 1) % 4) for dev in range(4)])]
    dot_general x0 -> x1, local copies, waits for them, and re-layouts: none -> 5.96 us  [per_device(): lax.dot_general(act_cols, grads_all, (((0,), (0,)), ((), ())), preferred_...]
    all_to_all x1, waiting for transfers between devices: 4.44 us -> 0.01 us  [per_device(): lax.all_to_all(send_rows, 'rep', split_axis=0, concat_axis=0, tiled=True)]
    ppermute x0 -> x3, starting transfers between devices: none -> 2.12 us  [per_device(): lax.ppermute(ring[-1], 'shard', [(dev, (dev + 1) % 4) for dev in range(4)])]
    unnamed x9 -> x16, local copies, waits for them, and re-layouts: 4.68 us -> 5.34 us
  transfers between devices with their start and end apart: 4 -> 7, of which waited for: 1 -> 2; matrix products, arithmetic and copies ran while one was open for 36% -> 51% of each run, Pallas kernels for 0% -> 0%
where the time goes in v1:
time: 111 us; the launch traced here: 110 us
  local copies, waits for them, and re-layouts  37.2 us (34%)
  starting transfers between devices  24.3 us (22%)
  other arithmetic  20.3 us (18%)
  waiting for transfers between devices  18.7 us (17%)
  matrix products  8.88 us (8%)
    ppermute x3, waiting for transfers between devices, per_device(): lax.ppermute(ring[-1], 'shard', [(dev, (dev + 1) % 4) for dev in range(4)])  18.5 us
    convert_element_type x1, other arithmetic, per_device(): (cleared + weight_grad.reshape(block_count, block_size)).astype(jnp.bfloa...  8.55 us
    all_to_all x1, starting transfers between devices, per_device(): lax.all_to_all(send_ids, 'rep', split_axis=0, concat_axis=0, tiled=True)  7.31 us
    scatter-add x1, other arithmetic, accumulate(): return blank.at[target].add(block_rows.astype(jnp.float32), mode='drop')  7.02 us
    reshape x1, local copies, waits for them, and re-layouts, per_device(): weight_grad.reshape(block_count, block_size)  6.47 us
    dot_general x1, local copies, waits for them, and re-layouts, per_device(): lax.dot_general(act_cols, grads_all, (((0,), (0,)), ((), ())), preferred_...  5.96 us
    all_to_all x1, starting transfers between devices, per_device(): lax.all_to_all(send_rows, 'rep', split_axis=0, concat_axis=0, tiled=True)  5.79 us
    dot_general x1, matrix products, per_device(): lax.dot_general(act_cols, grads_all, (((0,), (0,)), ((), ())), preferred_...  5.67 us
  transfers between devices with their start and end apart: 7, of which 2 were waited for; matrix products, arithmetic and copies ran while one was open for 51% of the time, Pallas kernels for 0%

profile of v1, /device:TPU:0, one launch (start us, length us, event | category | flops | bytes accessed | tf_op | source)
XLA Modules:
  0.0 110.2 jit_solution(6701992643124041882)
XLA Ops:
  0.6 0.0 copy-start
  0.6 1.0 reduce-window.4
  1.6 0.7 fusion.13
  2.3 0.8 convert_reduce_fusion.1
  3.1 0.3 convert_reduce_fusion
  3.3 3.2 %scatter_custom_fusion.1 = s32[1024]{0:T(1024)} fusion(s32[512]{0:T(512)S(1)} %bitcast.56, s32[512]{0:T(512)} %bitcast.54, s32[]{:T(128)} %constant.58.clone.1), kind=kCustom, calls=%fused_computation.37 | custom fusion | bytes 4608 | tf_op jit(solution)/shard_map/scatter | solution.py:60
  6.5 7.3 %all-to-all-start.2 = ((s32[8,128,1]{1,2,0:T(1,128)}), s32[8,128,1]{1,2,0:T(1,128)S(1)}, u32[]{:S(2)}, u32[]{:S(2)}) async-start(s32[8,128,1]{1,2,0:T(1,128)} %bitcast.15), calls=%async_computation.2 | async-start | bytes 8192 | tf_op jit(solution)/shard_map/all_to_all | solution.py:63
  13.8 0.7 compare_select_fusion.2
  14.5 5.5 %scatter_custom_fusion.2 = bf16[1024,128]{1,0:T(8,128)(2,1)} fusion(s32[512]{0:T(512)S(1)} %bitcast.57, bf16[]{:T(256)} %constant.64.clone.1, bf16[10240,128]{1,0:T(8,128)(2,1)} %bitcast.43, s32[1024]{0:T(1024)S(1)} %pad_clamp_fusion), kind=kCustom, calls=%fused_computation.16 | custom fusion | bytes 262656 | tf_op jit(solution)/shard_map/scatter | solution.py:58
  20.0 0.2 all-to-all-done.2
  20.2 5.8 %all-to-all-start.3 = ((bf16[8,128,128]{2,1,0:T(8,128)(2,1)}), bf16[8,128,128]{2,1,0:T(8,128)(2,1)S(1)}, u32[]{:S(2)}, u32[]{:S(2)}) async-start(bf16[8,128,128]{2,1,0:T(8,128)(2,1)} %bitcast.24), calls=%async_computation.3 | async-start | bytes 524288 | tf_op jit(solution)/shard_map/all_to_all | solution.py:62
  26.0 0.0 collective-permute-start
  26.0 0.0 copy-start.3
  26.1 4.1 %copy.23 = bf16[128,8192]{0,1:T(8,128)(2,1)} copy(bf16[128,8192]{1,0:T(8,128)(2,1)} %param.6) | data formatting | bytes 4194304 | tf_op args[0]
  30.1 0.0 copy-done.3
  30.1 0.6 constant_dynamic-slice_fusion
  30.7 0.6 dynamic_slice.11
  31.3 2.5 %scatter_custom_fusion = pred[10240]{0:T(1024)(128)(4,1)S(1)} fusion(s32[512]{0:T(512)S(1)} %bitcast.51, pred[512]{0:T(512)(128)(4,1)S(1)} %broadcast.122, pred[]{:T(512)} %constant.54.clone.1), kind=kCustom, calls=%fused_computation.20 | custom fusion | bytes 10241 | tf_op jit(solution)/shard_map/scatter | solution.py:46
  33.8 0.0 collective-permute-done
  33.8 1.6 %collective-permute-start.1 = (bf16[128,640]{1,0:T(8,128)(2,1)S(1)}, bf16[128,640]{1,0:T(8,128)(2,1)S(1)}, u32[]{:S(2)}, u32[]{:S(2)}) collective-permute-start(bf16[128,640]{1,0:T(8,128)(2,1)S(1)} %collective-permute-done), channel_id=1, source_target_pairs={{0,1},{1,2},{2,3},{3,0},{4,5},{5,6},{6,7},{7,4},{8,9},{9,10},{10,1... | collective-permute-start | bytes 491528 | tf_op jit(solution)/shard_map/ppermute | solution.py:18
  35.4 0.0 all-to-all-done.3
  35.4 4.4 %all-to-all-start.1 = ((bf16[128,4,2048]{0,2,1:T(8,128)(2,1)}), bf16[128,4,2048]{0,2,1:T(8,128)(2,1)}, u32[]{:S(2)}, u32[]{:S(2)}) async-start(bf16[128,4,2048]{0,2,1:T(8,128)(2,1)} %bitcast.42), calls=%async_computation.1 | async-start | bytes 4194304 | tf_op jit(solution)/shard_map/all_to_all | solution.py:24
  39.9 0.0 copy-start.1
  39.9 0.7 broadcast_subtract_fusion
  40.6 0.0 collective-permute-done.1
  40.6 0.5 collective-permute-start.2
  41.1 0.6 compare_select_fusion
  41.7 7.0 %scatter_custom_fusion.3 = f32[1920,128]{1,0:T(8,128)} fusion(s32[1024]{0:T(1024)S(1)} %bitcast.55, bf16[1024,128]{1,0:T(8,128)(2,1)S(1)} %bitcast.46, f32[]{:T(128)} %constant.57.clone.1), kind=kCustom, calls=%fused_computation.13 | custom fusion | flops 262144 | bytes 1245188 | tf_op jit(solution)/shard_map/scatter-add | solution.py:12
  48.7 18.5 %collective-permute-done.2 = bf16[128,640]{1,0:T(8,128)(2,1)S(1)} collective-permute-done((bf16[128,640]{1,0:T(8,128)(2,1)S(1)}, bf16[128,640]{1,0:T(8,128)(2,1)S(1)}, u32[]{:S(2)}, u32[]{:S(2)}) %collective-permute-start.2) | collective-permute-done | bytes 163872 | tf_op jit(solution)/shard_map/ppermute | solution.py:18
  67.3 0.0 copy-done.1
  67.5 0.0 copy-start.2
  67.5 1.1 copy-done.2
  68.6 0.0 copy-done
  68.6 3.2 %convolution_convert_fusion = bf16[512,2048]{1,0:T(8,128)(2,1)} fusion(bf16[2048,640]{1,0:T(8,128)(2,1)S(1)} %copy-done, bf16[1024,640]{1,0:T(8,128)(2,1)S(1)} %constant_dynamic-update-slice_fusion, s32[]{:T(128)S(6)} %select_n.66), kind=kOutput, calls=%fused_computation.7 | convolution fusion | flops 1343225856 | bytes 5373956 | tf_op jit(solution)/shard_map/dot_general | solution.py:28
  71.8 0.0 all-to-all-done.1
  71.8 4.7 %all-to-all-start = ((bf16[4,128,2048]{2,1,0:T(8,128)(2,1)}), bf16[4,128,2048]{2,1,0:T(8,128)(2,1)}, u32[]{:S(2)}, u32[]{:S(2)}) async-start(bf16[4,128,2048]{2,1,0:T(8,128)(2,1)} %bitcast.44), calls=%async_computation | async-start | bytes 4194304 | tf_op jit(solution)/shard_map/all_to_all | solution.py:31
  76.5 4.0 %copy.24 = bf16[4,128,2048]{2,1,0:T(8,128)(2,1)} copy(bf16[4,128,2048]{1,2,0:T(8,128)(2,1)} %bitcast.5) | data formatting | bytes 4194304 | tf_op jit(solution)/shard_map/all_to_all | solution.py:24
  80.4 5.7 %convolution_bitcast_fusion = f32[2048,640]{0,1:T(8,128)} fusion(bf16[512,2048]{1,0:T(8,128)(2,1)} %bitcast.41, bf16[1024,640]{1,0:T(8,128)(2,1)} %copy-done.2, s32[]{:T(128)S(6)} %select_n.66), kind=kOutput, calls=%fused_computation.6 | convolution fusion | flops 1342177280 | bytes 7995396 | tf_op jit(solution)/shard_map/dot_general | solution.py:25
  86.1 6.0 %copy.25 = f32[2048,640]{1,0:T(8,128)} copy(f32[2048,640]{0,1:T(8,128)} %convolution_bitcast_fusion) | data formatting | bytes 10485760 | tf_op jit(solution)/shard_map/dot_general | solution.py:25
  92.1 6.5 %reshape.138 = f32[1,10240,128]{2,1,0:T(8,128)} reshape(f32[2048,640]{1,0:T(8,128)} %copy.25) | data formatting | bytes 10485760 | tf_op jit(solution)/shard_map/reshape | solution.py:48
  98.5 8.5 %add_convert_fusion = bf16[1,10240,128]{2,1,0:T(8,128)(2,1)} fusion(f32[1,10240,128]{2,1,0:T(8,128)} %reshape.138, bf16[1,10240,128]{2,1,0:T(8,128)(2,1)} %param.9, pred[10240]{0:T(1024)(128)(4,1)S(1)} %scatter_custom_fusion), kind=kLoop, calls=%fused_computation.5 | loop fusion | flops 5242880 | bytes 10496000 | tf_op jit(solution)/shard_map/convert_element_type | solution.py:48
  107.1 0.0 all-to-all-done
  107.1 3.2 %copy.28 = bf16[4,16,8,2048]{3,2,0,1:T(8,128)(2,1)} copy(bf16[4,16,8,2048]{3,2,1,0:T(8,128)(2,1)} %bitcast.29) | data formatting | bytes 4194304 | tf_op jit(solution)/shard_map/all_to_all | solution.py:31
  (14 shorter events, 0.2 us)
Async XLA Ops:
  0.6 68.0 %copy-start = (bf16[2048,640]{1,0:T(8,128)(2,1)S(1)}, bf16[2048,640]{1,0:T(8,128)(2,1)}, u32[]{:S(2)}) copy-start(bf16[2048,640]{1,0:T(8,128)(2,1)} %param.8) | copy-start | bytes 7864324
  6.5 13.7 %all-to-all-start.2 = ((s32[8,128,1]{1,2,0:T(1,128)}), s32[8,128,1]{1,2,0:T(1,128)S(1)}, u32[]{:S(2)}, u32[]{:S(2)}) async-start(s32[8,128,1]{1,2,0:T(1,128)} %bitcast.15), calls=%async_computation.2 | async-start | bytes 8192 | tf_op jit(solution)/shard_map/all_to_all | solution.py:63
  20.2 15.2 %all-to-all-start.3 = ((bf16[8,128,128]{2,1,0:T(8,128)(2,1)}), bf16[8,128,128]{2,1,0:T(8,128)(2,1)S(1)}, u32[]{:S(2)}, u32[]{:S(2)}) async-start(bf16[8,128,128]{2,1,0:T(8,128)(2,1)} %bitcast.24), calls=%async_computation.3 | async-start | bytes 524288 | tf_op jit(solution)/shard_map/all_to_all | solution.py:62
  26.0 7.8 %collective-permute-start = (bf16[128,640]{1,0:T(8,128)(2,1)}, bf16[128,640]{1,0:T(8,128)(2,1)S(1)}, u32[]{:S(2)}, u32[]{:S(2)}) collective-permute-start(bf16[128,640]{1,0:T(8,128)(2,1)} %param.7), channel_id=1, source_target_pairs={{0,1},{1,2},{2,3},{3,0},{4,5},{5,6},{6,7},{7,4},{8,9},{9,10},{10,1... | collective-permute-start | bytes 491528 | tf_op jit(solution)/shard_map/ppermute | solution.py:18
  26.0 4.1 %copy-start.3 = (s32[1,8]{1,0:T(1,128)S(1)}, s32[1,8]{1,0:T(1,128)}, u32[]{:S(2)}) copy-start(s32[1,8]{1,0:T(1,128)} %param.11) | copy-start | bytes 100
  33.8 6.8 %collective-permute-start.1 = (bf16[128,640]{1,0:T(8,128)(2,1)S(1)}, bf16[128,640]{1,0:T(8,128)(2,1)S(1)}, u32[]{:S(2)}, u32[]{:S(2)}) collective-permute-start(bf16[128,640]{1,0:T(8,128)(2,1)S(1)} %collective-permute-done), channel_id=1, source_target_pairs={{0,1},{1,2},{2,3},{3,0},{4,5},{5,6},{6,7},{7,4},{8,9},{9,10},{10,1... | collective-permute-start | bytes 491528 | tf_op jit(solution)/shard_map/ppermute | solution.py:18
  35.4 36.4 %all-to-all-start.1 = ((bf16[128,4,2048]{0,2,1:T(8,128)(2,1)}), bf16[128,4,2048]{0,2,1:T(8,128)(2,1)}, u32[]{:S(2)}, u32[]{:S(2)}) async-start(bf16[128,4,2048]{0,2,1:T(8,128)(2,1)} %bitcast.42), calls=%async_computation.1 | async-start | bytes 4194304 | tf_op jit(solution)/shard_map/all_to_all | solution.py:24
  39.9 27.5 %copy-start.1 = (bf16[128,640]{1,0:T(8,128)(2,1)S(1)}, bf16[128,640]{1,0:T(8,128)(2,1)}, u32[]{:S(2)}) copy-start(bf16[128,640]{1,0:T(8,128)(2,1)} %param.7) | copy-start | bytes 491524
  40.6 26.7 %collective-permute-start.2 = (bf16[128,640]{1,0:T(8,128)(2,1)S(1)}, bf16[128,640]{1,0:T(8,128)(2,1)S(1)}, u32[]{:S(2)}, u32[]{:S(2)}) collective-permute-start(bf16[128,640]{1,0:T(8,128)(2,1)S(1)} %collective-permute-done.1), channel_id=1, source_target_pairs={{0,1},{1,2},{2,3},{3,0},{4,5},{5,6},{6,7},{7,4},{8,9},{9,10},{10,1... | collective-permute-start | bytes 491528 | tf_op jit(solution)/shard_map/ppermute | solution.py:18
  67.5 1.1 copy-start.2
  71.8 35.3 %all-to-all-start = ((bf16[4,128,2048]{2,1,0:T(8,128)(2,1)}), bf16[4,128,2048]{2,1,0:T(8,128)(2,1)}, u32[]{:S(2)}, u32[]{:S(2)}) async-start(bf16[4,128,2048]{2,1,0:T(8,128)(2,1)} %bitcast.44), calls=%async_computation | async-start | bytes 4194304 | tf_op jit(solution)/shard_map/all_to_all | solution.py:31
